TPU v7x, 32 devices: a whole 2x2x4 slice. The times are simulated.
32 devices in a mesh: dp: 1, tp: 32 (over x, y, z, core).
Axes of the slice: x: 2, y: 2, z: 4, core: 2. Of those that a mesh axis runs over, the one named last changes fastest.
Arguments:
- x: bfloat16 [2048, 5120], P('dp')
- dy: bfloat16 [2048, 5120], P('dp')
- gate: bfloat16 [2048, 12288], P('dp', 'tp')
- up: bfloat16 [2048, 12288], P('dp', 'tp')
- w_gate: bfloat16 [5120, 12288], P(None, 'tp')
- w_up: bfloat16 [5120, 12288], P(None, 'tp')
- w_down: bfloat16 [12288, 5120], P('tp')
Outputs:
- output 1: bfloat16 [2048, 5120], P('dp')
- output 2: bfloat16 [5120, 12288], P('dp', 'tp')
- output 3: bfloat16 [5120, 12288], P('dp', 'tp')
- output 4: bfloat16 [12288, 5120], P(('dp', 'tp'))
All inputs are finite; a program needn't handle non-finite values.
Results may differ from a plain program's by a relative error of at most 0.012.
Values are sent between devices in bfloat16 or wider.
A program may use at most 2 GiB of HBM per device.

v0:
```python
import jax
import jax.numpy as jnp
from jax import lax
from jax.sharding import PartitionSpec as P


def act(gate, up):
    return jax.nn.silu(gate) * up


def solution(mesh):
    def step(x, dy, gate, up, w_gate, w_up, w_down):
        hidden, back = jax.vjp(act, gate.astype(jnp.float32), up.astype(jnp.float32))
        d_hidden = jnp.dot(dy, w_down.T, preferred_element_type=jnp.float32)
        d_gate, d_up = (g.astype(jnp.bfloat16) for g in back(d_hidden))
        term = jnp.dot(d_gate, w_gate.T, preferred_element_type=jnp.float32) + jnp.dot(d_up, w_up.T, preferred_element_type=jnp.float32)
        dx = lax.psum(term.astype(jnp.bfloat16), "tp")
        dw_gate = jnp.dot(x.T, d_gate, preferred_element_type=jnp.float32)
        dw_up = jnp.dot(x.T, d_up, preferred_element_type=jnp.float32)
        dw_down = jnp.dot(hidden.astype(jnp.bfloat16).T, dy, preferred_element_type=jnp.float32)
        return dx, *(g.astype(jnp.bfloat16) for g in (dw_gate, dw_up, dw_down))

    tokens, columns, rows = P("dp", None), P(None, "tp"), P("tp", None)
    return jax.shard_map(
        step,
        mesh=mesh,
        in_specs=(tokens, tokens, P("dp", "tp"), P("dp", "tp"), columns, columns, rows),
        out_specs=(tokens, P("dp", "tp"), P("dp", "tp"), P(("dp", "tp"), None)),
        check_vma=False,
    )
```

profile of v0, /device:TPU:0, one launch (start us, length us, event | category | flops | bytes accessed | tf_op | source)
XLA Modules:
  0.0 427.1 jit_solution(8274579397126446830)
XLA Ops:
  7.2 0.0 all-reduce.2.cloned.1.call-start
  7.2 18.6 %fusion.8 = (bf16[2048,384]{1,0:T(8,128)(2,1)}, f32[2048,384]{1,0:T(8,128)S(1)}) fusion(bf16[2048,384]{1,0:T(8,128)(2,1)} %param.9, bf16[2048,384]{1,0:T(8,128)(2,1)} %param.10, bf16[2048,5120]{1,0:T(8,128)(2,1)} %param.8, bf16[384,5120]{1,0:T(8,128)(2,1)} %param.13), kind=kOutput, calls=%fused_computation.18 | convolution fusion | flops 8063287296 | bytes 32768000 | tf_op jit(solution)/shard_map/dot_general | solution.py:14
  25.9 0.0 copy-start
  25.9 21.2 %fusion.11 = f32[2048,5120]{1,0:T(8,128)} fusion(bf16[2048,384]{1,0:T(8,128)(2,1)} %get-tuple-element.8, bf16[5120,384]{1,0:T(8,128)(2,1)} %param.11), kind=kOutput, calls=%fused_computation.21 | convolution fusion | flops 8053063680 | bytes 47448064 | tf_op jit(solution)/shard_map/dot_general | solution.py:16
  47.0 0.0 copy-done
  47.0 24.1 %add_convert_fusion = bf16[2048,5120]{1,0:T(8,128)(2,1)} fusion(f32[2048,5120]{1,0:T(8,128)} %fusion.11, bf16[5120,384]{1,0:T(8,128)(2,1)} %param.12, f32[2048,384]{1,0:T(8,128)S(1)} %get-tuple-element.9, bf16[2048,384]{1,0:T(8,128)(2,1)S(1)} %copy-done), kind=kOutput, calls=%fused_computation | convolution fusion | flops 8079540224 | bytes 71565312 | tf_op jit(solution)/shard_map/dot_general | solution.py:16
  71.1 0.0 all-reduce.2.cloned.1.call-update
  71.1 14.5 %fusion = bf16[5120,384]{0,1:T(8,128)(2,1)} fusion(bf16[2048,384]{1,0:T(8,128)(2,1)} %get-tuple-element.8, bf16[2048,5120]{1,0:T(8,128)(2,1)} %param.7), kind=kOutput, calls=%fused_computation.4 | convolution fusion | flops 8055029760 | bytes 26476544 | tf_op jit(solution)/shard_map/dot_general | solution.py:18
  85.6 6.3 %copy.11 = bf16[5120,384]{1,0:T(8,128)(2,1)} copy(bf16[5120,384]{0,1:T(8,128)(2,1)} %fusion) | data formatting | bytes 7864320
  91.9 14.6 %fusion.1 = bf16[5120,384]{0,1:T(8,128)(2,1)} fusion(bf16[2048,5120]{1,0:T(8,128)(2,1)} %param.7, f32[2048,384]{1,0:T(8,128)S(1)} %get-tuple-element.9, bf16[2048,384]{1,0:T(8,128)(2,1)} %param.9), kind=kOutput, calls=%fused_computation.5 | convolution fusion | flops 8060534784 | bytes 29622272 | tf_op jit(solution)/shard_map/dot_general | solution.py:19
  106.5 0.0 copy-start.1
  106.5 0.0 copy-start.2
  106.5 6.4 %copy.12 = bf16[5120,384]{1,0:T(8,128)(2,1)} copy(bf16[5120,384]{0,1:T(8,128)(2,1)} %fusion.1) | data formatting | bytes 7864320
  112.9 0.0 copy-done.1
  112.9 0.0 copy-done.2
  112.9 14.7 %convolution_convert_fusion = bf16[384,5120]{1,0:T(8,128)(2,1)} fusion(bf16[2048,5120]{1,0:T(8,128)(2,1)} %param.8, bf16[2048,384]{1,0:T(8,128)(2,1)S(1)} %copy-done.2, bf16[2048,384]{1,0:T(8,128)(2,1)S(1)} %copy-done.1), kind=kOutput, calls=%fused_computation.1 | convolution fusion | flops 8061321216 | bytes 28049408 | tf_op jit(solution)/shard_map/dot_general | solution.py:20
  127.6 275.4 %all-reduce.2.cloned.1.call-done = bf16[2048,5120]{1,0:T(8,128)(2,1)} async-done(((bf16[2048,5120]{1,0:T(8,128)(2,1)}), bf16[2048,5120]{1,0:T(8,128)(2,1)}) %all-reduce.2.cloned.1.call-update) | async-done | bytes 20971536 | tf_op jit(solution)/shard_map/psum | solution.py:17
  403.0 17.3 %copy.14 = bf16[2048,5120]{1,0:T(8,128)(2,1)} copy(bf16[2048,5120]{1,0:T(8,128)(2,1)} %all-reduce.2.cloned.1.call-done) | data formatting | bytes 41943040
Async XLA Ops:
  7.2 395.8 %all-reduce.2.cloned.1.call-start = ((), (), s32[]{:S(2)}) async-start(), calls=%async_computation | async-start | bytes 41943040 | tf_op jit(solution)/shard_map/psum | solution.py:17
  25.9 21.2 %copy-start = (bf16[2048,384]{1,0:T(8,128)(2,1)S(1)}, bf16[2048,384]{1,0:T(8,128)(2,1)}, u32[]{:S(2)}) copy-start(bf16[2048,384]{1,0:T(8,128)(2,1)} %param.9) | copy-start | bytes 4718596
  106.5 6.4 %copy-start.1 = (bf16[2048,384]{1,0:T(8,128)(2,1)S(1)}, bf16[2048,384]{1,0:T(8,128)(2,1)}, u32[]{:S(2)}) copy-start(bf16[2048,384]{1,0:T(8,128)(2,1)} %param.9) | copy-start | bytes 4718596
  106.5 6.4 %copy-start.2 = (bf16[2048,384]{1,0:T(8,128)(2,1)S(1)}, bf16[2048,384]{1,0:T(8,128)(2,1)}, u32[]{:S(2)}) copy-start(bf16[2048,384]{1,0:T(8,128)(2,1)} %param.10) | copy-start | bytes 4718596
Sparse Core Ops, SparseCore 0:
  71.3 331.6 all-reduce.1
where the time goes:
time: 428 us; the launch traced here: 427 us
  waiting for transfers between devices  275 us (64%)
  matrix products  108 us (25%)
  local copies, waits for them, and re-layouts  30 us (7%)
  between operations  14 us (3%)
    psum x1, waiting for transfers between devices, step(): dx = lax.psum(term.astype(jnp.bfloat16), 'tp')  275 us
    unnamed x9, local copies, waits for them, and re-layouts  30 us
    dot_general x1, matrix products, step(): jnp.dot(d_up, w_up.T, preferred_element_type=jnp.float32)  24.1 us
    dot_general x1, matrix products, step(): jnp.dot(d_gate, w_gate.T, preferred_element_type=jnp.float32)  21.2 us
    dot_general x1, matrix products, step(): d_hidden = jnp.dot(dy, w_down.T, preferred_element_type=jnp.float32)  18.6 us
    dot_general x1, matrix products, step(): jnp.dot(hidden.astype(jnp.bfloat16).T, dy, preferred_element_type=jnp.flo...  14.7 us
    dot_general x1, matrix products, step(): dw_up = jnp.dot(x.T, d_up, preferred_element_type=jnp.float32)  14.6 us
    dot_general x1, matrix products, step(): dw_gate = jnp.dot(x.T, d_gate, preferred_element_type=jnp.float32)  14.5 us
  transfers between devices with their start and end apart: 1, of which 1 were waited for; matrix products, arithmetic and copies ran while one was open for 13% of the time, Pallas kernels for 0%

commit v1 on v0

v1 whole, which is shorter than its diff:
```python
import jax
import jax.numpy as jnp
from jax import lax
from jax.experimental import pallas as pl
from jax.experimental.pallas import tpu as pltpu
from jax.sharding import PartitionSpec as P

MESH = pl.DeviceIdType.MESH
R = 1024


class Comm:
    def __init__(self, G, D, cw, pA=320, KS=None):
        self.G, self.D, self.cw = G, D, cw
        self.K = KS or 3 * D
        self.a = pA; self.h = pA // 2; self.q = pA // 4
        self.e = R - 2 * pA; self.b = self.e // 4
        assert self.q % 16 == 0 and self.b % 16 == 0
        self.NS = 10
        self.rx = dict(A0=self.h, B0=self.h, A1=self.q, B1=self.q, A2=self.q, B2=self.q, A3=self.q, B3=self.q,
                       E0=3*self.b, E1=2*self.b, E2=self.b, EX=self.b, EY=self.b)
        off = 0; self.off = {}
        for k, v in self.rx.items():
            self.off[k] = off; off += v
        self.rxrows = off
        self.kinds = {}
        for i in range(8):
            self.kinds['A%d' % i] = len(self.kinds); self.kinds['B%d' % i] = len(self.kinds)
        for i in range(9):
            self.kinds['E%d' % i] = len(self.kinds)
        self.kinds['D'] = len(self.kinds); self.kinds['L'] = len(self.kinds)

    def scratch(self):
        n = len(self.kinds)
        return [pltpu.VMEM((self.G, R, self.cw), jnp.bfloat16),
                pltpu.VMEM((self.K, self.rxrows, self.cw), jnp.bfloat16),
                pltpu.SemaphoreType.DMA((n, self.K)), pltpu.SemaphoreType.DMA((n, self.K)), pltpu.SemaphoreType.REGULAR]

    def bind(self, work, rxb, ssem, rsem, credit, out):
        self.work, self.rxb, self.ssem, self.rsem, self.credit, self.out = work, rxb, ssem, rsem, credit, out
        me = lax.axis_index("tp")
        core = me % 2; z = (me // 2) % 4; y = (me // 8) % 2; x = me // 16
        idx = lambda x, y, z, c: ((x * 2 + y) * 4 + z) * 2 + c
        self.core, self.z, self.y, self.x = core, z, y, x
        side = z // 2; self.side = side
        self.outer = jnp.logical_or(z == 0, z == 3); self.inner = jnp.logical_not(self.outer)
        zi = 1 + side
        zo = 3 * side
        self.px = idx(1 - x, y, z, core); self.py = idx(x, 1 - y, z, core)
        self.pc = idx(x, y, z, 1 - core)
        self.pin = idx(x, y, zi, core)
        self.pout = idx(x, y, zo, core)
        self.pacr = idx(x, y, 2 - side, core)
        m = lambda v: pl.multiple_of(v, 16)
        a, h, q, b = self.a, self.h, self.q, self.b
        e0 = 2 * a
        self.Ak = m(x * h); self.As = m((1 - x) * h)
        self.Aq = m(x * h + y * q); self.Aqs = m(x * h + (1 - y) * q)
        self.Bk = m(a + y * h); self.Bs = m(a + (1 - y) * h)
        self.Bq = m(a + y * h + x * q); self.Bqs = m(a + y * h + (1 - x) * q)
        self.Eex = m(e0 + (1 - side) * b); self.Efar = m(e0 + (1 - side) * 2 * b); self.Enear = m(e0 + side * 2 * b)
        self.Eown = m(e0 + z * b); self.Eout = m(e0 + zo * b)

    def barrier(self):
        bar = pltpu.get_barrier_semaphore()
        def sig(d): pl.semaphore_signal(bar, inc=1, device_id={"tp": d}, device_id_type=MESH)
        sig(self.px); sig(self.py); sig(self.pc)
        @pl.when(self.outer)
        def _(): sig(self.pin); pl.semaphore_wait(bar, 4)
        @pl.when(self.inner)
        def _(): sig(self.pout); sig(self.pacr); pl.semaphore_wait(bar, 5)

    def cp(self, kind, c, start, rows, dst_kind, dev):
        k = self.kinds[kind]; sl = c % self.K
        src = self.work.at[c, pl.ds(start, rows), :]
        if dst_kind is None: dst = src
        else: dst = self.rxb.at[sl, pl.ds(self.off[dst_kind], rows), :]
        return pltpu.make_async_remote_copy(src_ref=src, dst_ref=dst, send_sem=self.ssem.at[k, sl], recv_sem=self.rsem.at[k, sl],
                                            device_id={"tp": dev}, device_id_type=MESH)

    def add(self, c, start, rows, rxk, roff=0):
        sl = c % self.K
        w = self.work.at[c, pl.ds(start, rows), :]
        v = w[...].astype(jnp.float32) + self.rxb[sl, pl.ds(self.off[rxk] + roff, rows), :].astype(jnp.float32)
        w[...] = v.astype(jnp.bfloat16)

    def stage(self, s, c):
        q, h, b = self.q, self.h, self.b
        C = self.cp
        A = [lambda: C('A0', c, self.As, h, 'A0', self.px), lambda: C('A1', c, self.Aqs, q, 'A1', self.py),
             lambda: C('A2', c, self.Aq, q, 'A2', self.pin), lambda: C('A3', c, self.Aq, q, 'A3', self.pacr),
             lambda: C('A4', c, self.Aq, q, None, self.pout), lambda: C('A5', c, self.Aq, q, None, self.py),
             lambda: C('A6', c, self.Ak, h, None, self.px)]
        B = [lambda: C('B0', c, self.Bs, h, 'B0', self.py), lambda: C('B1', c, self.Bqs, q, 'B1', self.px),
             lambda: C('B2', c, self.Bq, q, 'B2', self.pin), lambda: C('B3', c, self.Bq, q, 'B3', self.pacr),
             lambda: C('B4', c, self.Bq, q, None, self.pout), lambda: C('B5', c, self.Bq, q, None, self.px),
             lambda: C('B6', c, self.Bk, h, None, self.py)]
        E = [lambda: C('E0', c, self.Eex, 3*b, 'E0', self.pin), lambda: C('E1', c, self.Efar, 2*b, 'E1', self.pacr),
             lambda: C('E2', c, self.Eout, b, 'E2', self.pout), lambda: C('E3', c, self.Eown, b, 'EX', self.px),
             lambda: C('E4', c, self.Eown, b, 'EY', self.py), lambda: C('E5', c, self.Eown, b, None, self.pin),
             lambda: C('E6', c, self.Enear, 2*b, None, self.pacr), lambda: C('E7', c, self.Eex, 3*b, None, self.pout)]
        ws = lambda d: d().wait_send()
        wr = lambda d: d().wait_recv()
        st = lambda d: d().start()
        outer = lambda f: pl.when(self.outer)(f)
        inner = lambda f: pl.when(self.inner)(f)
        if s == 0:
            st(A[0]); st(B[0])
            @outer
            def _(): st(E[0])
        elif s == 1:
            @inner
            def _(): wr(E[0]); self.add(c, self.Eex, 3*b, 'E0'); st(E[1])
            @outer
            def _(): ws(E[0])
            A[0]().wait(); self.add(c, self.Ak, h, 'A0'); st(A[1])
            B[0]().wait(); self.add(c, self.Bk, h, 'B0'); st(B[1])
        elif s == 2:
            @inner
            def _(): E[1]().wait(); self.add(c, self.Enear, 2*b, 'E1'); st(E[2])
            A[1]().wait(); self.add(c, self.Aq, q, 'A1')
            @outer
            def _(): st(A[2])
            B[1]().wait(); self.add(c, self.Bq, q, 'B1')
            @outer
            def _(): st(B[2])
        elif s == 3:
            @inner
            def _():
                ws(E[2])
                wr(A[2]); self.add(c, self.Aq, q, 'A2'); st(A[3])
                wr(B[2]); self.add(c, self.Bq, q, 'B2'); st(B[3])
            @outer
            def _(): wr(E[2]); self.add(c, self.Eown, b, 'E2'); ws(A[2]); ws(B[2]); pl.semaphore_signal(self.credit, inc=1, device_id={"tp": self.pin}, device_id_type=MESH)
            st(E[3])
        elif s == 4:
            @inner
            def _():
                pl.semaphore_wait(self.credit, 1)
                A[3]().wait(); self.add(c, self.Aq, q, 'A3'); st(A[4])
                B[3]().wait(); self.add(c, self.Bq, q, 'B3'); st(B[4])
            E[3]().wait(); self.add(c, self.Eown, b, 'EX'); st(E[4])
        elif s == 5:
            E[4]().wait(); self.add(c, self.Eown, b, 'EY')
            @outer
            def _(): wr(A[4]); wr(B[4]); st(E[5])
            @inner
            def _(): ws(A[4])
            st(A[5])
            @inner
            def _(): ws(B[4])
            st(B[5])
        elif s == 6:
            @inner
            def _(): wr(E[5]); st(E[6])
            @outer
            def _(): ws(E[5])
            A[5]().wait(); st(A[6])
            B[5]().wait(); st(B[6])
        elif s == 7:
            @inner
            def _(): E[6]().wait(); st(E[7])
            A[6]().wait(); B[6]().wait()
        elif s == 8:
            @inner
            def _(): ws(E[7])
            @outer
            def _(): wr(E[7])
            d, l = self.final(c); d.start(); l.start()
        elif s == 9:
            d, l = self.final(c); d.wait(); l.wait()

    def final(self, c):
        sl = c % self.K
        dst = self.out.at[pl.ds(pl.multiple_of(self.core * R, R), R), pl.ds(pl.multiple_of(c * self.cw, self.cw), self.cw)]
        src = self.work.at[c]
        k = self.kinds['D']; k2 = self.kinds['L']
        d = pltpu.make_async_remote_copy(src_ref=src, dst_ref=dst, send_sem=self.ssem.at[k, sl], recv_sem=self.rsem.at[k, sl],
                                         device_id={"tp": self.pc}, device_id_type=MESH)
        l = pltpu.make_async_copy(src, dst, self.ssem.at[k2, sl])
        return d, l

    def tick(self, t):
        for s in reversed(range(self.NS)):
            c = t - self.D * s
            @pl.when(jnp.logical_and(c >= 0, c < self.G))
            def _(s=s, c=c): self.stage(s, c)
    @property
    def nticks(self): return self.G + self.D * (self.NS - 1)


T, D, F = 2048, 5120, 384
G, SPACING, CW = 40, 2, 128
RB = 256
NB = T // RB
UW = 256
NU = D // UW
PIECES = 5
UNIT0 = 5


def nt(a, b):
    return lax.dot_general(a, b, (((1,), (1,)), ((), ())), preferred_element_type=jnp.float32)


def nn(a, b):
    return jnp.dot(a, b, preferred_element_type=jnp.float32)


def kernel(comm, x, dy, gate, up, w_gate, w_up, w_down, dx, dwg, dwu, dwd,
           work, rxb, ssem, rsem, credit, wown, wfar, dall, dfar, dall_t, hid_t,
           own_sem, far_s, far_r, df_s, df_r):
    comm.bind(work, rxb, ssem, rsem, credit, dx)
    mine = pl.multiple_of(comm.core * R, R)
    theirs = pl.multiple_of((1 - comm.core) * R, R)
    own = [pltpu.make_async_copy(w, wown.at[:, pl.ds(i * F, F)], own_sem.at[i]) for i, w in enumerate((w_gate, w_up))]
    PR = D // PIECES

    def far(i, p):
        rows = pl.ds(pl.multiple_of(p * PR, PR), PR)
        return pltpu.make_async_remote_copy(
            src_ref=(w_gate, w_up)[i].at[rows], dst_ref=wfar.at[rows, pl.ds(i * F, F)], send_sem=far_s.at[i, p],
            recv_sem=far_r.at[i, p], device_id={"tp": comm.pc}, device_id_type=MESH)

    def dsend(b):
        return pltpu.make_async_remote_copy(
            src_ref=dall.at[pl.ds(pl.multiple_of(theirs + b * RB, RB), RB)],
            dst_ref=dfar.at[pl.ds(pl.multiple_of(b * RB, RB), RB)], send_sem=df_s.at[b], recv_sem=df_r.at[b],
            device_id={"tp": comm.pc}, device_id_type=MESH)

    def hidden_part(wd, dyb, gb, ub, sem):
        pre = [pltpu.make_async_copy(s, d, sem.at[2 + i]) for i, (s, d) in enumerate(((w_down, wd), (gate, gb), (up, ub)))]

        def row0(b):
            return pl.multiple_of(lax.rem(theirs + b * RB, T), RB)

        def load(b):
            return pltpu.make_async_copy(dy.at[pl.ds(row0(b), RB)], dyb.at[lax.rem(b, 2)], sem.at[lax.rem(b, 2)])

        load(0).start()
        for c in pre:
            c.start()
        comm.barrier()
        for p in range(PIECES):
            for i in range(2):
                far(i, p).start()
        for c in own:
            c.start()
        for c in pre:
            c.wait()

        def step(b, _):
            @pl.when(b + 1 < NB)
            def _():
                load(b + 1).start()
            load(b).wait()
            rows = pl.ds(row0(b), RB)
            dh = nt(dyb[lax.rem(b, 2)], wd[...])
            g, u = gb[rows, :].astype(jnp.float32), ub[rows, :].astype(jnp.float32)
            sig = jax.nn.sigmoid(g)
            silu = g * sig
            d_up = (dh * silu).astype(jnp.bfloat16)
            d_gate = (dh * u * (sig + silu * (1.0 - sig))).astype(jnp.bfloat16)
            hid = (silu * u).astype(jnp.bfloat16)
            dall[rows, 0:F] = d_gate
            dall[rows, F:2 * F] = d_up
            dall_t[0:F, rows] = d_gate.T
            dall_t[F:2 * F, rows] = d_up.T
            hid_t[:, rows] = hid.T

            @pl.when(b < NB // 2)
            def _():
                dsend(b).start()
            return 0

        lax.fori_loop(0, NB, step, 0)

    pl.run_scoped(hidden_part, pltpu.VMEM((F, D), jnp.bfloat16), pltpu.VMEM((2, RB, D), jnp.bfloat16),
                  pltpu.VMEM((T, F), jnp.bfloat16), pltpu.VMEM((T, F), jnp.bfloat16), pltpu.SemaphoreType.DMA((5,)))

    def terms(pair):
        per = PR // (2 * CW)

        @pl.when(lax.rem(pair, per) == 0)
        def _():
            for i in range(2):
                far(i, pair // per).wait()
        rows = pl.ds(pl.multiple_of(pair * 2 * CW, 2 * CW), 2 * CW)
        for half in range(2):
            r = pl.ds(half * R // 2, R // 2)
            t = nt(dall[pl.ds(pl.multiple_of(mine + half * R // 2, R // 2), R // 2), :], wown[rows, :]) + nt(dfar[r, :], wfar[rows, :])
            t = t.astype(jnp.bfloat16)
            work[2 * pair, r, :] = t[:, :CW]
            work[2 * pair + 1, r, :] = t[:, CW:]

    def main_part(xb, dyb, og, od, lsem, osem):
        def loads(u):
            s = lax.rem(u, 2)
            cols = pl.ds(pl.multiple_of(u * UW, UW), UW)
            return [pltpu.make_async_copy(x.at[:, cols], xb.at[s], lsem.at[0, s]),
                    pltpu.make_async_copy(dy.at[:, cols], dyb.at[s], lsem.at[1, s])]

        def stores(u):
            s = lax.rem(u, 2)
            cols = pl.ds(pl.multiple_of(u * UW, UW), UW)
            return [pltpu.make_async_copy(og.at[s, 0], dwg.at[cols], osem.at[0, s]),
                    pltpu.make_async_copy(og.at[s, 1], dwu.at[cols], osem.at[1, s]),
                    pltpu.make_async_copy(od.at[s], dwd.at[:, cols], osem.at[2, s])]

        for c in loads(0):
            c.start()
        for b in range(NB // 2):
            dsend(b).wait()
        for c in own:
            c.wait()
        terms(0)

        def unit(u):
            s = lax.rem(u, 2)

            @pl.when(u + 1 < NU)
            def _():
                for c in loads(u + 1):
                    c.start()
            for c in loads(u):
                c.wait()

            @pl.when(u >= 2)
            def _():
                for c in stores(u - 2):
                    c.wait()
            for i in range(2):
                og[s, i] = nn(dall_t[pl.ds(i * F, F), :], xb[s]).T.astype(jnp.bfloat16)
            od[s] = nn(hid_t[...], dyb[s]).astype(jnp.bfloat16)
            for c in stores(u):
                c.start()

        def tick(t, _):
            comm.tick(t)
            pair = t // 2 + 1

            @pl.when(jnp.logical_and(lax.rem(t, 2) == 0, pair < G // 2))
            def _():
                terms(pair)
            u = (t - UNIT0) // 2

            @pl.when(jnp.logical_and(jnp.logical_and(t >= UNIT0, lax.rem(t - UNIT0, 2) == 0), u < NU))
            def _():
                unit(u)
            return 0

        lax.fori_loop(0, comm.nticks, tick, 0)
        for u in (NU - 2, NU - 1):
            for c in stores(u):
                c.wait()

    pl.run_scoped(main_part, pltpu.VMEM((2, T, UW), jnp.bfloat16), pltpu.VMEM((2, T, UW), jnp.bfloat16),
                  pltpu.VMEM((2, 2, UW, F), jnp.bfloat16), pltpu.VMEM((2, F, UW), jnp.bfloat16),
                  pltpu.SemaphoreType.DMA((2, 2)), pltpu.SemaphoreType.DMA((3, 2)))


def solution(mesh):
    def step(x, dy, gate, up, w_gate, w_up, w_down):
        comm = Comm(G, SPACING, CW)
        bf = jnp.bfloat16
        any_ = pl.BlockSpec(memory_space=pl.ANY)
        dma = pltpu.SemaphoreType.DMA
        return pl.pallas_call(
            lambda *refs: kernel(comm, *refs),
            name="mlp_backward",
            out_shape=[jax.ShapeDtypeStruct(s, bf) for s in ((T, D), (D, F), (D, F), (F, D))],
            in_specs=[any_] * 7,
            out_specs=[any_] * 4,
            scratch_shapes=comm.scratch() + [
                pltpu.VMEM((D, 2 * F), bf), pltpu.VMEM((D, 2 * F), bf), pltpu.VMEM((T, 2 * F), bf), pltpu.VMEM((R, 2 * F), bf),
                pltpu.VMEM((2 * F, T), bf), pltpu.VMEM((F, T), bf),
                dma((2,)), dma((2, PIECES)), dma((2, PIECES)), dma((NB // 2,)), dma((NB // 2,))],
            compiler_params=pltpu.CompilerParams(collective_id=0, has_side_effects=True, vmem_limit_bytes=67043328),
        )(x, dy, gate, up, w_gate, w_up, w_down)

    tokens, columns, rows = P("dp", None), P(None, "tp"), P("tp", None)
    return jax.shard_map(
        step,
        mesh=mesh,
        in_specs=(tokens, tokens, P("dp", "tp"), P("dp", "tp"), columns, columns, rows),
        out_specs=(tokens, P("dp", "tp"), P("dp", "tp"), P(("dp", "tp"), None)),
        check_vma=False,
    )
```

time: 428 us -> 201 us (0.47)
  waiting for transfers between devices: 275 us -> 0 us
  Pallas kernels: 0 us -> 174 us
  matrix products: 108 us -> 0 us
  between operations: 14 us -> 0.65 us
    psum x1 -> x0, waiting for transfers between devices: 275 us -> none  [step(): dx = lax.psum(term.astype(jnp.bfloat16), 'tp')]
    pallas_call x0 -> x1, Pallas kernels: none -> 174 us  [step(): pl.pallas_call(lambda *refs: kernel(comm, *refs), name='mlp_backward', ou...]
    dot_general x6 -> x0, matrix products: 108 us -> none  [the longest x1 24.1 us: step(): jnp.dot(d_up, w_up.T, preferred_element_type=jnp.float32)]
    unnamed x9 -> x10, local copies, waits for them, and re-layouts: 30 us -> 26.6 us
  transfers between devices with their start and end apart: 1 -> 0, of which waited for: 1 -> 0; matrix products, arithmetic and copies ran while one was open for 13% -> 0% of each run, Pallas kernels for 0% -> 0%
where the time goes in v1:
time: 201 us
  Pallas kernels  174 us (87%)
  local copies, waits for them, and re-layouts  26.6 us (13%)
    pallas_call x1, Pallas kernels, step(): pl.pallas_call(lambda *refs: kernel(comm, *refs), name='mlp_backward', ou...  174 us
    unnamed x10, local copies, waits for them, and re-layouts  26.6 us

profile of v1, /device:TPU:0, one launch (start us, length us, event | category | flops | bytes accessed | tf_op | source)
XLA Modules:
  0.0 200.8 jit_solution(12452980297691742989)
XLA Ops:
  0.6 173.6 %mlp_backward.1 = (bf16[2048,5120]{1,0:T(8,128)(2,1)}, bf16[5120,384]{1,0:T(8,128)(2,1)}, bf16[5120,384]{1,0:T(8,128)(2,1)}, bf16[384,5120]{1,0:T(8,128)(2,1)}) custom-call(bf16[2048,5120]{1,0:T(8,128)(2,1)} %refs_0_.1, bf16[2048,5120]{1,0:T(8,128)(2,1)} %refs_1_.1, bf16[2048,384]{1,0:T(8,128)(2,1)} %refs_2_.1, bf16[2048,384]{1,0:T(8,128)(2,1)} %refs_3_.1, ...), custom_call_target="tpu_custom_call" | custom-call | tf_op jit(solution)/shard_map/mlp_backward/pallas_call | solution.py:368
  174.2 0.0 copy-start.2
  174.2 17.6 %copy.15 = bf16[2048,5120]{1,0:T(8,128)(2,1)} copy(bf16[2048,5120]{1,0:T(8,128)(2,1)} %get-tuple-element.8) | data formatting | bytes 41943040
  191.8 0.0 copy-done.2
  191.8 0.0 copy-start.1
  191.8 2.0 copy.16
  193.8 1.5 copy-done.1
  195.3 0.0 copy-start
  195.3 2.0 copy.17
  197.3 1.5 copy-done
  198.8 1.9 copy.18
Async XLA Ops:
  174.2 17.6 %copy-start.2 = (bf16[5120,384]{1,0:T(8,128)(2,1)S(1)}, bf16[5120,384]{1,0:T(8,128)(2,1)}, u32[]{:S(2)}) copy-start(bf16[5120,384]{1,0:T(8,128)(2,1)} %get-tuple-element.9) | copy-start | bytes 11796484
  191.8 3.5 %copy-start.1 = (bf16[5120,384]{1,0:T(8,128)(2,1)S(1)}, bf16[5120,384]{1,0:T(8,128)(2,1)}, u32[]{:S(2)}) copy-start(bf16[5120,384]{1,0:T(8,128)(2,1)} %get-tuple-element.10) | copy-start | bytes 11796484
  195.3 3.5 %copy-start = (bf16[384,5120]{1,0:T(8,128)(2,1)S(1)}, bf16[384,5120]{1,0:T(8,128)(2,1)}, u32[]{:S(2)}) copy-start(bf16[384,5120]{1,0:T(8,128)(2,1)} %get-tuple-element.11) | copy-start | bytes 11796484

commit v2 on v1

--- a/solution.py
+++ b/solution.py
@@ -28,16 +28,15 @@
             self.kinds['A%d' % i] = len(self.kinds); self.kinds['B%d' % i] = len(self.kinds)
         for i in range(9):
             self.kinds['E%d' % i] = len(self.kinds)
-        self.kinds['D'] = len(self.kinds); self.kinds['L'] = len(self.kinds)
+        self.kinds['D'] = len(self.kinds)
 
     def scratch(self):
         n = len(self.kinds)
-        return [pltpu.VMEM((self.G, R, self.cw), jnp.bfloat16),
-                pltpu.VMEM((self.K, self.rxrows, self.cw), jnp.bfloat16),
+        return [pltpu.VMEM((self.K, self.rxrows, self.cw), jnp.bfloat16),
                 pltpu.SemaphoreType.DMA((n, self.K)), pltpu.SemaphoreType.DMA((n, self.K)), pltpu.SemaphoreType.REGULAR]
 
-    def bind(self, work, rxb, ssem, rsem, credit, out):
-        self.work, self.rxb, self.ssem, self.rsem, self.credit, self.out = work, rxb, ssem, rsem, credit, out
+    def bind(self, work, other, rxb, ssem, rsem, credit):
+        self.work, self.other, self.rxb, self.ssem, self.rsem, self.credit = work, other, rxb, ssem, rsem, credit
         me = lax.axis_index("tp")
         core = me % 2; z = (me // 2) % 4; y = (me // 8) % 2; x = me // 16
         idx = lambda x, y, z, c: ((x * 2 + y) * 4 + z) * 2 + c
@@ -74,6 +73,7 @@
         k = self.kinds[kind]; sl = c % self.K
         src = self.work.at[c, pl.ds(start, rows), :]
         if dst_kind is None: dst = src
+        elif dst_kind == 'other': dst = self.other.at[c]
         else: dst = self.rxb.at[sl, pl.ds(self.off[dst_kind], rows), :]
         return pltpu.make_async_remote_copy(src_ref=src, dst_ref=dst, send_sem=self.ssem.at[k, sl], recv_sem=self.rsem.at[k, sl],
                                             device_id={"tp": dev}, device_id_type=MESH)
@@ -166,19 +166,9 @@
             def _(): ws(E[7])
             @outer
             def _(): wr(E[7])
-            d, l = self.final(c); d.start(); l.start()
+            st(lambda: C('D', c, 0, R, 'other', self.pc))
         elif s == 9:
-            d, l = self.final(c); d.wait(); l.wait()
-
-    def final(self, c):
-        sl = c % self.K
-        dst = self.out.at[pl.ds(pl.multiple_of(self.core * R, R), R), pl.ds(pl.multiple_of(c * self.cw, self.cw), self.cw)]
-        src = self.work.at[c]
-        k = self.kinds['D']; k2 = self.kinds['L']
-        d = pltpu.make_async_remote_copy(src_ref=src, dst_ref=dst, send_sem=self.ssem.at[k, sl], recv_sem=self.rsem.at[k, sl],
-                                         device_id={"tp": self.pc}, device_id_type=MESH)
-        l = pltpu.make_async_copy(src, dst, self.ssem.at[k2, sl])
-        return d, l
+            C('D', c, 0, R, 'other', self.pc).wait()
 
     def tick(self, t):
         for s in reversed(range(self.NS)):
@@ -207,10 +197,9 @@
     return jnp.dot(a, b, preferred_element_type=jnp.float32)
 
 
-def kernel(comm, x, dy, gate, up, w_gate, w_up, w_down, dx, dwg, dwu, dwd,
-           work, rxb, ssem, rsem, credit, wown, wfar, dall, dfar, dall_t, hid_t,
-           own_sem, far_s, far_r, df_s, df_r):
-    comm.bind(work, rxb, ssem, rsem, credit, dx)
+def kernel(comm, x, dy, gate, up, w_gate, w_up, w_down, wown, wfar, work, other,
+           rxb, ssem, rsem, credit, dall, dfar, dall_t, hid_t, own_sem, far_s, far_r, df_s, df_r):
+    comm.bind(work, other, rxb, ssem, rsem, credit)
     mine = pl.multiple_of(comm.core * R, R)
     theirs = pl.multiple_of((1 - comm.core) * R, R)
     own = [pltpu.make_async_copy(w, wown.at[:, pl.ds(i * F, F)], own_sem.at[i]) for i, w in enumerate((w_gate, w_up))]
@@ -229,16 +218,17 @@
             device_id={"tp": comm.pc}, device_id_type=MESH)
 
     def hidden_part(wd, dyb, gb, ub, sem):
-        pre = [pltpu.make_async_copy(s, d, sem.at[2 + i]) for i, (s, d) in enumerate(((w_down, wd), (gate, gb), (up, ub)))]
+        wd_copy = pltpu.make_async_copy(w_down, wd, sem.at[3, 0])
 
         def row0(b):
             return pl.multiple_of(lax.rem(theirs + b * RB, T), RB)
 
         def load(b):
-            return pltpu.make_async_copy(dy.at[pl.ds(row0(b), RB)], dyb.at[lax.rem(b, 2)], sem.at[lax.rem(b, 2)])
-
-        load(0).start()
-        for c in pre:
+            rows, s = pl.ds(row0(b), RB), lax.rem(b, 2)
+            return [pltpu.make_async_copy(a.at[rows], v.at[s], sem.at[i, s]) for i, (a, v) in enumerate(((dy, dyb), (gate, gb), (up, ub)))]
+
+        wd_copy.start()
+        for c in load(0):
             c.start()
         comm.barrier()
         for p in range(PIECES):
@@ -246,17 +236,18 @@
                 far(i, p).start()
         for c in own:
             c.start()
-        for c in pre:
-            c.wait()
+        wd_copy.wait()
 
         def step(b, _):
             @pl.when(b + 1 < NB)
             def _():
-                load(b + 1).start()
-            load(b).wait()
-            rows = pl.ds(row0(b), RB)
-            dh = nt(dyb[lax.rem(b, 2)], wd[...])
-            g, u = gb[rows, :].astype(jnp.float32), ub[rows, :].astype(jnp.float32)
+                for c in load(b + 1):
+                    c.start()
+            for c in load(b):
+                c.wait()
+            rows, s = pl.ds(row0(b), RB), lax.rem(b, 2)
+            dh = nt(dyb[s], wd[...])
+            g, u = gb[s].astype(jnp.float32), ub[s].astype(jnp.float32)
             sig = jax.nn.sigmoid(g)
             silu = g * sig
             d_up = (dh * silu).astype(jnp.bfloat16)
@@ -276,7 +267,7 @@
         lax.fori_loop(0, NB, step, 0)
 
     pl.run_scoped(hidden_part, pltpu.VMEM((F, D), jnp.bfloat16), pltpu.VMEM((2, RB, D), jnp.bfloat16),
-                  pltpu.VMEM((T, F), jnp.bfloat16), pltpu.VMEM((T, F), jnp.bfloat16), pltpu.SemaphoreType.DMA((5,)))
+                  pltpu.VMEM((2, RB, F), jnp.bfloat16), pltpu.VMEM((2, RB, F), jnp.bfloat16), pltpu.SemaphoreType.DMA((4, 2)))
 
     def terms(pair):
         per = PR // (2 * CW)
@@ -288,24 +279,18 @@
         rows = pl.ds(pl.multiple_of(pair * 2 * CW, 2 * CW), 2 * CW)
         for half in range(2):
             r = pl.ds(half * R // 2, R // 2)
-            t = nt(dall[pl.ds(pl.multiple_of(mine + half * R // 2, R // 2), R // 2), :], wown[rows, :]) + nt(dfar[r, :], wfar[rows, :])
+            m = pl.ds(pl.multiple_of(mine + half * R // 2, R // 2), R // 2)
+            t = nt(dall[m, :], wown[rows, :]) + nt(dfar[r, :], wfar[rows, :])
             t = t.astype(jnp.bfloat16)
             work[2 * pair, r, :] = t[:, :CW]
             work[2 * pair + 1, r, :] = t[:, CW:]
 
-    def main_part(xb, dyb, og, od, lsem, osem):
+    def main_part(xb, dyb, lsem):
         def loads(u):
             s = lax.rem(u, 2)
             cols = pl.ds(pl.multiple_of(u * UW, UW), UW)
             return [pltpu.make_async_copy(x.at[:, cols], xb.at[s], lsem.at[0, s]),
                     pltpu.make_async_copy(dy.at[:, cols], dyb.at[s], lsem.at[1, s])]
-
-        def stores(u):
-            s = lax.rem(u, 2)
-            cols = pl.ds(pl.multiple_of(u * UW, UW), UW)
-            return [pltpu.make_async_copy(og.at[s, 0], dwg.at[cols], osem.at[0, s]),
-                    pltpu.make_async_copy(og.at[s, 1], dwu.at[cols], osem.at[1, s]),
-                    pltpu.make_async_copy(od.at[s], dwd.at[:, cols], osem.at[2, s])]
 
         for c in loads(0):
             c.start()
@@ -325,15 +310,10 @@
             for c in loads(u):
                 c.wait()
 
-            @pl.when(u >= 2)
-            def _():
-                for c in stores(u - 2):
-                    c.wait()
+            rows = pl.ds(pl.multiple_of(u * UW, UW), UW)
             for i in range(2):
-                og[s, i] = nn(dall_t[pl.ds(i * F, F), :], xb[s]).T.astype(jnp.bfloat16)
-            od[s] = nn(hid_t[...], dyb[s]).astype(jnp.bfloat16)
-            for c in stores(u):
-                c.start()
+                wown[rows, pl.ds(i * F, F)] = nn(dall_t[pl.ds(i * F, F), :], xb[s]).T.astype(jnp.bfloat16)
+            wfar[rows, 0:F] = nn(hid_t[...], dyb[s]).T.astype(jnp.bfloat16)
 
         def tick(t, _):
             comm.tick(t)
@@ -350,13 +330,34 @@
             return 0
 
         lax.fori_loop(0, comm.nticks, tick, 0)
-        for u in (NU - 2, NU - 1):
-            for c in stores(u):
-                c.wait()
-
-    pl.run_scoped(main_part, pltpu.VMEM((2, T, UW), jnp.bfloat16), pltpu.VMEM((2, T, UW), jnp.bfloat16),
-                  pltpu.VMEM((2, 2, UW, F), jnp.bfloat16), pltpu.VMEM((2, F, UW), jnp.bfloat16),
-                  pltpu.SemaphoreType.DMA((2, 2)), pltpu.SemaphoreType.DMA((3, 2)))
+
+    pl.run_scoped(main_part, pltpu.VMEM((2, T, UW), jnp.bfloat16), pltpu.VMEM((2, T, UW), jnp.bfloat16), pltpu.SemaphoreType.DMA((2, 2)))
+
+
+def write_out(dw, dwd_t, work, other, dx, dwg, dwu, dwd, stage, sem_x, sem_w, sem_d):
+    copies = [pltpu.make_async_copy(dw.at[:, pl.ds(i * F, F)], o, sem_w.at[i]) for i, o in enumerate((dwg, dwu))]
+    core = lax.rem(lax.axis_index("tp"), 2)
+    for i, half in enumerate((work, other)):
+        rows = pl.ds(pl.multiple_of(R * (core if i == 0 else 1 - core), R), R)
+        copies += [pltpu.make_async_copy(half.at[c], dx.at[rows, pl.ds(c * CW, CW)], sem_x.at[i, c]) for c in range(G)]
+    for c in copies:
+        c.start()
+
+    def put(u):
+        s = lax.rem(u, 2)
+        return pltpu.make_async_copy(stage.at[s], dwd.at[:, pl.ds(pl.multiple_of(u * UW, UW), UW)], sem_d.at[s])
+
+    def flip(u, _):
+        @pl.when(u >= 2)
+        def _():
+            put(u - 2).wait()
+        stage[lax.rem(u, 2)] = dwd_t[pl.ds(pl.multiple_of(u * UW, UW), UW), 0:F].T
+        put(u).start()
+        return 0
+
+    lax.fori_loop(0, NU, flip, 0)
+    for c in copies + [put(NU - 2), put(NU - 1)]:
+        c.wait()
 
 
 def solution(mesh):
@@ -364,19 +365,28 @@
         comm = Comm(G, SPACING, CW)
         bf = jnp.bfloat16
         any_ = pl.BlockSpec(memory_space=pl.ANY)
+        vmem = pl.BlockSpec(memory_space=pltpu.VMEM)
         dma = pltpu.SemaphoreType.DMA
-        return pl.pallas_call(
+        held = pl.pallas_call(
             lambda *refs: kernel(comm, *refs),
             name="mlp_backward",
+            out_shape=[pltpu.VMEM(s, bf) for s in ((D, 2 * F), (D, 2 * F), (G, R, CW), (G, R, CW))],
+            in_specs=[any_] * 7,
+            out_specs=[vmem] * 4,
+            scratch_shapes=comm.scratch() + [
+                pltpu.VMEM((T, 2 * F), bf), pltpu.VMEM((R, 2 * F), bf), pltpu.VMEM((2 * F, T), bf), pltpu.VMEM((F, T), bf),
+                dma((2,)), dma((2, PIECES)), dma((2, PIECES)), dma((NB // 2,)), dma((NB // 2,))],
+            compiler_params=pltpu.CompilerParams(collective_id=0, has_side_effects=True, vmem_limit_bytes=26 * 2**20),
+        )(x, dy, gate, up, w_gate, w_up, w_down)
+        return pl.pallas_call(
+            write_out,
+            name="write_out",
             out_shape=[jax.ShapeDtypeStruct(s, bf) for s in ((T, D), (D, F), (D, F), (F, D))],
-            in_specs=[any_] * 7,
+            in_specs=[vmem] * 4,
             out_specs=[any_] * 4,
-            scratch_shapes=comm.scratch() + [
-                pltpu.VMEM((D, 2 * F), bf), pltpu.VMEM((D, 2 * F), bf), pltpu.VMEM((T, 2 * F), bf), pltpu.VMEM((R, 2 * F), bf),
-                pltpu.VMEM((2 * F, T), bf), pltpu.VMEM((F, T), bf),
-                dma((2,)), dma((2, PIECES)), dma((2, PIECES)), dma((NB // 2,)), dma((NB // 2,))],
-            compiler_params=pltpu.CompilerParams(collective_id=0, has_side_effects=True, vmem_limit_bytes=67043328),
-        )(x, dy, gate, up, w_gate, w_up, w_down)
+            scratch_shapes=[pltpu.VMEM((2, F, UW), bf), dma((2, G)), dma((2,)), dma((2,))],
+            compiler_params=pltpu.CompilerParams(vmem_limit_bytes=2**20),
+        )(*held)
 
     tokens, columns, rows = P("dp", None), P(None, "tp"), P("tp", None)
     return jax.shard_map(

time: 201 us -> 191 us (0.950)
  local copies, waits for them, and re-layouts: 26.6 us -> 0 us
  Pallas kernels: 174 us -> 190 us
    unnamed x10 -> x0, local copies, waits for them, and re-layouts: 26.6 us -> none
    pallas_call x0 -> x1, Pallas kernels: none -> 17.3 us  [step(): pl.pallas_call(write_out, name='write_out', out_shape=[jax.ShapeDtypeStru...]
where the time goes in v2:
time: 191 us
  Pallas kernels  190 us (99%)
    pallas_call x1, Pallas kernels, step(): pl.pallas_call(lambda *refs: kernel(comm, *refs), name='mlp_backward', ou...  173 us
    pallas_call x1, Pallas kernels, step(): pl.pallas_call(write_out, name='write_out', out_shape=[jax.ShapeDtypeStru...  17.3 us

profile of v2, /device:TPU:0, one launch (start us, length us, event | category | flops | bytes accessed | tf_op | source)
XLA Modules:
  0.0 190.7 jit_solution(17350217489427186676)
XLA Ops:
  0.6 172.8 %mlp_backward.1 = (bf16[5120,768]{1,0:T(8,128)(2,1)S(1)}, bf16[5120,768]{1,0:T(8,128)(2,1)S(1)}, bf16[40,1024,128]{2,1,0:T(8,128)(2,1)S(1)}, bf16[40,1024,128]{2,1,0:T(8,128)(2,1)S(1)}) custom-call(bf16[2048,5120]{1,0:T(8,128)(2,1)} %refs_0_.1, bf16[2048,5120]{1,0:T(8,128)(2,1)} %refs_1_.1, bf16[2048,384]{1,0:T(8,128)(2,1)} %refs_2_.1, ...), custom_call_target="tpu_custom_call" | custom-call | tf_op jit(solution)/shard_map/mlp_backward/pallas_call | solution.py:370
  173.4 17.3 %write_out.1 = (bf16[2048,5120]{1,0:T(8,128)(2,1)}, bf16[5120,384]{1,0:T(8,128)(2,1)}, bf16[5120,384]{1,0:T(8,128)(2,1)}, bf16[384,5120]{1,0:T(8,128)(2,1)}) custom-call(bf16[5120,768]{1,0:T(8,128)(2,1)S(1)} %get-tuple-element.8.dw, bf16[5120,768]{1,0:T(8,128)(2,1)S(1)} %get-tuple-element.9.dwd_t, bf16[40,1024,128]{2,1,0:T(8,128)(2,1)S(1)} %get-tuple-element.10.work, ...), custom_call_target="tpu_custom_call" | custom-call | tf_op jit(solution)/shard_map/write_out/pallas_call | solution.py:381
